TPU v7x, 8 devices: a whole 2x2x1 slice. The times are simulated.
8 devices in a mesh: dp: 2 (over z, y), pp: 4 (over x, core).
Axes of the slice: x: 2, y: 2, z: 1, core: 2. Of those that a mesh axis runs over, the one named last changes fastest.
Arguments:
- tok_ids: int32 [2, 2, 130], P(None, 'dp')
- emb_s: bfloat16 [4, 50304, 2048], P('pp', 'dp')
- w_one: bfloat16 [4, 1, 2048, 8192], P('pp')
- w_two: bfloat16 [4, 1, 8192, 2048], P('pp')
- gain_f: bfloat16 [2048], replicated
- gain_h: bfloat16 [2048], replicated
- gain_e: bfloat16 [2048], replicated
- gain_m: bfloat16 [2048], replicated
- w_proj: bfloat16 [4096, 2048], replicated
- u_one: bfloat16 [2048, 8192], replicated
- u_two: bfloat16 [8192, 2048], replicated
- w_out: bfloat16 [2048, 50304], replicated
Outputs:
- output 1: float32 [], replicated
- output 2: float32 [2, 2, 128], P(None, 'dp')
- output 3: float32 [2, 2, 128], P(None, 'dp')
All inputs are finite; a program needn't handle non-finite values.
Results may differ from a plain program's by a relative error of at most 0.00315102.
Values are sent between devices in bfloat16 or wider.
A program may use at most 1.75 GiB of HBM per device.

v0:
```python
import jax
import jax.numpy as jnp
from jax import lax
from jax.sharding import PartitionSpec as P

NORM_EPS = 1e-6
MTP_WEIGHT = 0.3
HEAD_ROWS = 128


def norm_plain(x_val):
    x_f = x_val.astype(jnp.float32)
    return (x_f * lax.rsqrt(jnp.mean(x_f * x_f, axis=-1, keepdims=True) + NORM_EPS)).astype(jnp.bfloat16)


def norm_gain(x_val, gain_vec):
    x_f = x_val.astype(jnp.float32)
    scaled = x_f * lax.rsqrt(jnp.mean(x_f * x_f, axis=-1, keepdims=True) + NORM_EPS)
    return (scaled * gain_vec.astype(jnp.float32)).astype(jnp.bfloat16)


def mlp_add(x_val, normed, w_up, w_down):
    hidden = jax.nn.gelu(jnp.dot(normed, w_up, preferred_element_type=jnp.float32)).astype(jnp.bfloat16)
    return (x_val.astype(jnp.float32) + jnp.dot(hidden, w_down, preferred_element_type=jnp.float32)).astype(jnp.bfloat16)


def mtp_depth(h_last, e_rows, gain_h, gain_e, gain_m, w_proj, u_one, u_two):
    row_width = h_last.shape[-1]
    z_sum = jnp.dot(norm_gain(h_last, gain_h), w_proj[:row_width], preferred_element_type=jnp.float32)
    z_sum = z_sum + jnp.dot(norm_gain(e_rows, gain_e), w_proj[row_width:], preferred_element_type=jnp.float32)
    z_val = z_sum.astype(jnp.bfloat16)
    return mlp_add(z_val, norm_gain(z_val, gain_m), u_one, u_two)


def token_nll(normed, targets, w_out):
    n_rows, row_width = normed.shape
    n_blocks = n_rows // HEAD_ROWS

    def one_block(pair):
        block_rows, block_tgt = pair
        logits = jnp.dot(block_rows, w_out, preferred_element_type=jnp.float32)
        picked = jnp.take_along_axis(logits, block_tgt[:, None], axis=1)[:, 0]
        return jax.nn.logsumexp(logits, axis=1) - picked

    per_block = lax.map(one_block, (normed.reshape(n_blocks, HEAD_ROWS, row_width), targets.reshape(n_blocks, HEAD_ROWS)))
    return per_block.reshape(n_rows)


def solution(mesh):
    n_stages = mesh.shape['pp']
    n_data = mesh.shape['dp']
    fwd_perm = [(stage_idx, stage_idx + 1) for stage_idx in range(n_stages - 1)]
    mtp_perm = [(0, n_stages - 1)]

    def body(tok_ids, emb_s, w_one, w_two, gain_f, gain_h, gain_e, gain_m, w_proj, u_one, u_two, w_out):
        stage = lax.axis_index('pp')
        n_micro, batch_dev, seq_plus = tok_ids.shape
        seq_len = seq_plus - 2
        n_layers = w_one.shape[1]
        row_width = w_one.shape[2]
        n_rows = batch_dev * seq_len
        is_first = stage == 0
        is_last = stage == n_stages - 1
        table = lax.all_gather(emb_s[0], 'dp', axis=0, tiled=True)

        def head_losses(h_last, e_rows, ids_out):
            main_nll = token_nll(norm_gain(h_last, gain_f), ids_out[:, 1:seq_len + 1].reshape(n_rows), w_out)
            z_val = mtp_depth(h_last, e_rows, gain_h, gain_e, gain_m, w_proj, u_one, u_two)
            mtp_nll = token_nll(norm_gain(z_val, gain_f), ids_out[:, 2:].reshape(n_rows), w_out)
            return main_nll, mtp_nll

        def no_losses(h_last, e_rows, ids_out):
            zero_rows = jnp.zeros((n_rows,), jnp.float32)
            return zero_rows, zero_rows

        def tick_step(state, t_idx):
            ids_in = lax.dynamic_index_in_dim(tok_ids, jnp.minimum(t_idx, n_micro - 1), axis=0, keepdims=False)
            out_idx = jnp.maximum(t_idx - (n_stages - 1), 0)
            ids_out = lax.dynamic_index_in_dim(tok_ids, out_idx, axis=0, keepdims=False)
            x_val = jnp.where(is_first, table[ids_in[:, :seq_len].reshape(n_rows)], state)
            for layer in range(n_layers):
                x_val = mlp_add(x_val, norm_plain(x_val), w_one[0, layer], w_two[0, layer])
            e_rows = lax.ppermute(table[ids_out[:, 1:seq_len + 1].reshape(n_rows)], 'pp', mtp_perm)
            losses = lax.cond(is_last & (t_idx >= n_stages - 1), head_losses, no_losses, x_val, e_rows, ids_out)
            return lax.ppermute(x_val, 'pp', fwd_perm), losses

        init_state = jnp.zeros((n_rows, row_width), jnp.bfloat16)
        _, (main_all, mtp_all) = lax.scan(tick_step, init_state, jnp.arange(n_micro + n_stages - 1))
        main_nll = lax.psum(main_all[n_stages - 1:], 'pp').reshape(n_micro, batch_dev, seq_len)
        mtp_nll = lax.psum(mtp_all[n_stages - 1:], 'pp').reshape(n_micro, batch_dev, seq_len)
        local_sum = jnp.sum(main_nll) + MTP_WEIGHT * jnp.sum(mtp_nll)
        total_loss = lax.psum(local_sum, 'dp') / (n_micro * batch_dev * n_data * seq_len)
        return total_loss, main_nll, mtp_nll

    replicated = P()
    in_specs = (P(None, 'dp', None), P('pp', 'dp', None), P('pp'), P('pp'), replicated, replicated, replicated, replicated, replicated, replicated, replicated, replicated)
    out_specs = (replicated, P(None, 'dp', None), P(None, 'dp', None))
    return jax.shard_map(body, mesh=mesh, in_specs=in_specs, out_specs=out_specs, check_vma=False)
```

profile of v0, /device:TPU:0, one launch (start us, length us, event | category | flops | bytes accessed | tf_op | source)
XLA Modules:
  0.0 3018.4 jit_solution(7960923983560915139)
XLA Ops:
  7.3 0.7 all-gather.3.cloned.1.call-update
  8.0 2332.2 %all-gather.3.cloned.1.call-done = bf16[1,50304,2048]{2,1,0:T(8,128)(2,1)} async-done(((bf16[1,25152,2048]{2,1,0:T(8,128)(2,1)}), bf16[1,50304,2048]{2,1,0:T(8,128)(2,1)}) %all-gather.3.cloned.1.call-update) | async-done | bytes 206045200 | tf_op jit(solution)/shard_map/all_gather | solution.py:64
  2340.7 0.8 broadcast_in_dim.47
  2341.5 442.8 %while.18 = (s32[]{:T(128)}, bf16[128,2048]{1,0:T(8,128)(2,1)}, f32[5,128]{1,0:T(8,128)}, f32[5,128]{1,0:T(8,128)}, pred[]{:T(512)}, /*index=5*/s32[5]{0:T(128)}...) while((s32[]{:T(128)}, bf16[128,2048]{1,0:T(8,128)(2,1)}, ...), condition=%wide.region_12.14_spmd, body=%wide.region_0.13_spmd.sunk | while | flops 72144502784 | bytes 684075008 | solution.py:88
  2341.6 1.2 dynamic_slice.35
  2344.1 0.8 dynamic-slice_bitcast_fusion.3
  2344.9 2.7 gather_fusion.3
  2347.7 2.6 collective-permute-start.1
  2350.3 2.7 gather_fusion.2
  2353.3 25.1 fusion.129
  2378.4 6.0 collective-permute-start
  2385.1 1.1 conditional.2
  2385.1 0.6 broadcast_in_dim.42
  2386.1 1.3 dynamic_update_slice.20
  2387.4 1.3 dynamic_update_slice.21
  2388.7 1.2 dynamic_slice.35
  2391.3 0.7 dynamic-slice_bitcast_fusion.3
  2392.1 2.7 gather_fusion.3
  2394.8 2.2 collective-permute-start.1
  2397.0 2.7 gather_fusion.2
  2400.0 25.1 fusion.129
  2425.1 9.8 collective-permute-start
  2435.6 1.1 conditional.2
  2435.6 0.6 broadcast_in_dim.42
  2436.6 1.3 dynamic_update_slice.20
  2437.9 1.3 dynamic_update_slice.21
  2439.2 1.2 dynamic_slice.35
  2441.8 0.7 dynamic-slice_bitcast_fusion.3
  2442.6 2.7 gather_fusion.3
  2445.3 1.3 collective-permute-start.1
  2446.6 2.7 gather_fusion.2
  2449.6 25.1 fusion.129
  2474.7 11.1 collective-permute-start
  2486.5 1.1 conditional.2
  2486.6 0.6 broadcast_in_dim.42
  2487.6 1.3 dynamic_update_slice.20
  2488.9 1.3 dynamic_update_slice.21
  2490.2 1.2 dynamic_slice.35
  2492.8 0.7 dynamic-slice_bitcast_fusion.3
  2493.5 2.7 gather_fusion.3
  2496.2 1.3 collective-permute-start.1
  2497.6 2.7 gather_fusion.2
  2500.6 25.1 fusion.129
  2525.7 11.1 collective-permute-start
  2537.5 1.1 conditional.2
  2537.5 0.6 broadcast_in_dim.42
  2538.6 1.3 dynamic_update_slice.20
  2539.9 1.3 dynamic_update_slice.21
  2541.2 1.2 dynamic_slice.35
  2543.7 0.8 dynamic-slice_bitcast_fusion.3
  2544.6 2.7 gather_fusion.3
  2547.3 202.5 %collective-permute-start.1 = (bf16[128,2048]{1,0:T(8,128)(2,1)S(1)}, bf16[128,2048]{1,0:T(8,128)(2,1)S(1)}, u32[]{:S(2)}, u32[]{:S(2)}) collective-permute-start(bf16[128,2048]{1,0:T(8,128)(2,1)S(1)} %gather_fusion.3), channel_id=1, source_target_pairs={{0,3},{4,7}} | collective-permute-start | bytes 1572872 | tf_op jit(solution)/shard_map/while/body/eval_jaxpr/ppermute | solution.py:83
  2749.8 2.7 gather_fusion.2
  2752.8 25.1 fusion.129
  2778.0 2.1 collective-permute-start
  2780.7 1.1 conditional.2
  2781.8 1.3 dynamic_update_slice.20
  2783.1 1.3 dynamic_update_slice.21
  2784.4 0.7 slice.30
  2785.1 0.7 slice.31
  2785.8 215.9 %all-reduce = (f32[2,128]{1,0:T(2,128)S(1)}, f32[2,128]{1,0:T(2,128)S(1)}) all-reduce(f32[2,128]{1,0:T(2,128)S(1)} %slice.30, f32[2,128]{1,0:T(2,128)S(1)} %slice.31), channel_id=1, replica_groups=mesh['dp'=2,'pp'=4] {'pp'}, use_global_device_ids=true, to_apply=%region_13.15 | all-reduce | flops 512 | bytes 4096 | tf_op jit(solution)/shard_map/psum | solution.py:89
  3001.7 0.7 reduce_sum.91
  3002.4 0.6 reduce_sum.90
  3004.3 5.4 psum.23
  (57 shorter events, 5.6 us)
Async XLA Ops:
  7.2 2334.4 %copy-start = (bf16[2048]{0:T(1024)(128)(2,1)S(1)}, bf16[2048]{0:T(1024)(128)(2,1)}, u32[]{:S(2)}) copy-start(bf16[2048]{0:T(1024)(128)(2,1)} %param.22) | copy-start | bytes 12292
  7.2 2334.4 %copy-start.1 = (bf16[2048]{0:T(1024)(128)(2,1)S(1)}, bf16[2048]{0:T(1024)(128)(2,1)}, u32[]{:S(2)}) copy-start(bf16[2048]{0:T(1024)(128)(2,1)} %param.23) | copy-start | bytes 12292
  7.2 2334.4 %copy-start.2 = (bf16[2048]{0:T(1024)(128)(2,1)S(1)}, bf16[2048]{0:T(1024)(128)(2,1)}, u32[]{:S(2)}) copy-start(bf16[2048]{0:T(1024)(128)(2,1)} %param.24) | copy-start | bytes 12292
  7.2 2334.3 %copy-start.3 = (bf16[2048]{0:T(1024)(128)(2,1)S(1)}, bf16[2048]{0:T(1024)(128)(2,1)}, u32[]{:S(2)}) copy-start(bf16[2048]{0:T(1024)(128)(2,1)} %param.25) | copy-start | bytes 12292
  7.2 2333.0 %all-gather.3.cloned.1.call-start = ((), (), s32[]{:S(2)}) async-start(), calls=%async_computation | async-start | bytes 309067776 | tf_op jit(solution)/shard_map/all_gather | solution.py:64
  2347.7 37.4 %collective-permute-start.1 = (bf16[128,2048]{1,0:T(8,128)(2,1)S(1)}, bf16[128,2048]{1,0:T(8,128)(2,1)S(1)}, u32[]{:S(2)}, u32[]{:S(2)}) collective-permute-start(bf16[128,2048]{1,0:T(8,128)(2,1)S(1)} %gather_fusion.3), channel_id=1, source_target_pairs={{0,3},{4,7}} | collective-permute-start | bytes 1572872 | tf_op jit(solution)/shard_map/while/body/eval_jaxpr/ppermute | solution.py:83
  2378.4 10.3 collective-permute-start
  2394.8 40.8 %collective-permute-start.1 = (bf16[128,2048]{1,0:T(8,128)(2,1)S(1)}, bf16[128,2048]{1,0:T(8,128)(2,1)S(1)}, u32[]{:S(2)}, u32[]{:S(2)}) collective-permute-start(bf16[128,2048]{1,0:T(8,128)(2,1)S(1)} %gather_fusion.3), channel_id=1, source_target_pairs={{0,3},{4,7}} | collective-permute-start | bytes 1572872 | tf_op jit(solution)/shard_map/while/body/eval_jaxpr/ppermute | solution.py:83
  2425.1 14.1 collective-permute-start
  2445.3 41.3 %collective-permute-start.1 = (bf16[128,2048]{1,0:T(8,128)(2,1)S(1)}, bf16[128,2048]{1,0:T(8,128)(2,1)S(1)}, u32[]{:S(2)}, u32[]{:S(2)}) collective-permute-start(bf16[128,2048]{1,0:T(8,128)(2,1)S(1)} %gather_fusion.3), channel_id=1, source_target_pairs={{0,3},{4,7}} | collective-permute-start | bytes 1572872 | tf_op jit(solution)/shard_map/while/body/eval_jaxpr/ppermute | solution.py:83
  2474.7 15.5 collective-permute-start
  2496.2 41.3 %collective-permute-start.1 = (bf16[128,2048]{1,0:T(8,128)(2,1)S(1)}, bf16[128,2048]{1,0:T(8,128)(2,1)S(1)}, u32[]{:S(2)}, u32[]{:S(2)}) collective-permute-start(bf16[128,2048]{1,0:T(8,128)(2,1)S(1)} %gather_fusion.3), channel_id=1, source_target_pairs={{0,3},{4,7}} | collective-permute-start | bytes 1572872 | tf_op jit(solution)/shard_map/while/body/eval_jaxpr/ppermute | solution.py:83
  2525.7 15.5 collective-permute-start
  2547.3 233.4 %collective-permute-start.1 = (bf16[128,2048]{1,0:T(8,128)(2,1)S(1)}, bf16[128,2048]{1,0:T(8,128)(2,1)S(1)}, u32[]{:S(2)}, u32[]{:S(2)}) collective-permute-start(bf16[128,2048]{1,0:T(8,128)(2,1)S(1)} %gather_fusion.3), channel_id=1, source_target_pairs={{0,3},{4,7}} | collective-permute-start | bytes 1572872 | tf_op jit(solution)/shard_map/while/body/eval_jaxpr/ppermute | solution.py:83
  2778.0 6.4 collective-permute-start
  3001.7 8.7 copy-start.4
  3001.7 8.7 copy-start.5
Sparse Core Ops, SparseCore 0:
  9.5 2330.6 all-gather.2
where the time goes:
time: 3020 us
  waiting for transfers between devices  2330 us (77%)
  starting transfers between devices  250 us (8%)
  blocking collectives  221 us (7%)
  matrix products  126 us (4%)
  local copies, waits for them, and re-layouts  57.9 us (2%)
    all_gather x1, waiting for transfers between devices, body(): table = lax.all_gather(emb_s[0], 'dp', axis=0, tiled=True)  2330 us
    psum x1, blocking collectives, body(): lax.psum(main_all[n_stages - 1:], 'pp').reshape(n_micro, batch_dev, seq_len)  216 us
    ppermute x5, starting transfers between devices, tick_step(): lax.ppermute(table[ids_out[:, 1:seq_len + 1].reshape(n_rows)], 'pp', mtp_...  210 us
    dot_general x5, matrix products, mlp_add(): jnp.dot(hidden, w_down, preferred_element_type=jnp.float32)  126 us
  transfers between devices with their start and end apart: 11, of which 1 were waited for; matrix products, arithmetic and copies ran while one was open for 5% of the time, Pallas kernels for 0%

commit v1 on v0

v1 whole, which is shorter than its diff:
```python
import functools

import jax
import jax.numpy as jnp
from jax import lax
from jax.experimental import pallas as pl
from jax.experimental.pallas import tpu as pltpu
from jax.sharding import PartitionSpec as P

NORM_EPS = 1e-6
MTP_WEIGHT = 0.3
LANES = 128
NEG = -3.0e38
CHUNK = 1024
HALF = 512
N_SLOTS = 12
MESH = pl.DeviceIdType.MESH
GROUP = 8


def gather_kernel(n_ids, flag_ref, grp_ref, sel_ref, table_ref, out_ref, buf, sems):
    n_batches = buf.shape[0]

    def start(batch):
        def one(j, carry):
            first = pl.multiple_of(grp_ref[batch * n_ids + j] * GROUP, GROUP)
            pltpu.make_async_copy(
                table_ref.at[pl.ds(first, GROUP), :], buf.at[batch, j], sems.at[batch]
            ).start()
            return carry

        lax.fori_loop(0, n_ids, one, 0, unroll=43)

    @pl.when(flag_ref[0] == 0)
    def _():
        for batch in range(n_batches):
            start(batch)
        col = lax.broadcasted_iota(jnp.int32, (out_ref.shape[1], n_ids * GROUP), 1)
        for batch in range(n_batches):
            pltpu.make_async_copy(buf.at[batch], buf.at[batch], sems.at[batch]).wait()
            hot = jnp.where(col == sel_ref[batch], 1.0, 0.0).astype(jnp.bfloat16)
            rows = buf[batch].reshape(n_ids * GROUP, -1)
            out_ref[batch] = jnp.dot(hot, rows, preferred_element_type=jnp.float32).astype(jnp.bfloat16)


def gather_rows(flag, local, owned, table):
    n_batches, n_ids = local.shape
    n_out = pl.cdiv(n_ids, GROUP) * GROUP
    width = table.shape[1]
    grp = local // GROUP
    sub = local - grp * GROUP
    sel = jnp.where(owned, jnp.arange(n_ids, dtype=jnp.int32) * GROUP + sub, -1)
    sel = jnp.pad(sel, ((0, 0), (0, n_out - n_ids)), constant_values=-1)
    return pl.pallas_call(
        functools.partial(gather_kernel, n_ids),
        grid_spec=pltpu.PrefetchScalarGridSpec(
            num_scalar_prefetch=2,
            grid=(),
            in_specs=[pl.BlockSpec(memory_space=pltpu.VMEM), pl.BlockSpec(memory_space=pl.ANY)],
            out_specs=pl.BlockSpec(memory_space=pltpu.VMEM),
            scratch_shapes=[
                pltpu.VMEM((n_batches, n_ids, GROUP, width), table.dtype),
                pltpu.SemaphoreType.DMA((n_batches,)),
            ],
        ),
        out_shape=jax.ShapeDtypeStruct((n_batches, n_out, width), table.dtype),
        compiler_params=pltpu.CompilerParams(vmem_limit_bytes=40 << 20),
        name="gather_rows",
    )(flag.reshape(1), grp.reshape(-1), sel[..., None], table)


def scaled_rows(rows, gain):
    x_f = rows.astype(jnp.float32)
    y = x_f * lax.rsqrt(jnp.mean(x_f * x_f, axis=-1, keepdims=True) + NORM_EPS)
    if gain is not None:
        y = y * gain
    return y.astype(jnp.bfloat16)


def norm_into(dst, src, gain_ref=None):
    gain = None if gain_ref is None else gain_ref[...].astype(jnp.float32).reshape(1, -1)
    for r in range(0, src.shape[0], 16):
        dst[pl.ds(r, 16), :] = scaled_rows(src[pl.ds(r, 16), :], gain)


def gelu(y):
    inner = y * (0.7978845608028654 + (0.7978845608028654 * 0.044715) * (y * y))
    return (y * (0.5 + 0.5 * jnp.tanh(inner))).astype(jnp.bfloat16)


def dot(a, b):
    return jnp.dot(a, b, preferred_element_type=jnp.float32)


def mega_kernel(
    rows, tgt, gain_f, gain_h, gain_e, gain_m, w_one, w_two, w_proj, u_one, u_two, w_out,
    out, wbuf, x_in, hid, x_out, h_buf, e_buf, n_buf, top, total, pick, stat,
    wsem, loc_sem, xs_sem, xr_sem, ex_s, ex_r, es_sem, er_sem, hs_sem, hs2_sem, hr_sem, rl_sem, zs_sem, zs2_sem, zr_sem, zl_sem, ss_sem, sr_sem,
):
    role = lax.axis_index('pp')
    dp = lax.axis_index('dp')
    n_roles, n_data = 4, 2
    n_dev = n_roles * n_data
    me = dp * n_roles + role
    n_vocab = w_out.shape[1]
    width = x_in.shape[2]
    n_half = n_buf.shape[1] // 2
    n_rows = n_buf.shape[1]
    n_cols = pl.cdiv(n_vocab, CHUNK)
    xn = n_buf.at[0, pl.ds(0, n_half)]
    body_rows = pl.ds(0, n_half)
    z_buf = x_in
    last_role = n_roles - 1
    last = role == last_role
    lane_main = jnp.where(role == 0, 0, jnp.where(role == 2, 1, 2))
    n_main = jnp.where(last, 0, (n_cols - lane_main + 2) // 3)
    n_mtp = (n_cols - role + 3) // 4
    q_mtp = jnp.where(last, 20, n_main)
    q_end = q_mtp + n_mtp

    def load(src, slot):
        pltpu.make_async_copy(src, wbuf.at[slot], wsem.at[slot]).start()

    def wait_slot(slot):
        pltpu.make_async_copy(w_proj.at[pl.ds(0, width), pl.ds(0, CHUNK)], wbuf.at[slot], wsem.at[slot]).wait()

    def cols(c):
        return pl.ds(pl.multiple_of(c * CHUNK, CHUNK), CHUNK)

    def rows_at(k):
        return pl.ds(pl.multiple_of(k * width, width), width)

    def up_chunk(c):
        return w_one.at[0, 0, :, cols(c)]

    def down_chunk(g, k):
        return w_two.at[0, 0, rows_at(k), cols(g)]

    def head_col(q):
        return jnp.where(q < n_main, lane_main + 3 * q, role + 4 * (q - q_mtp))

    def head_start(col):
        return pl.multiple_of(jnp.minimum(col * CHUNK, n_vocab - CHUNK), LANES)

    def issue_post(q):
        slot = lax.rem(q, N_SLOTS)

        @pl.when(((q < n_main) | (q >= q_mtp)) & (q < q_end))
        def _():
            load(w_out.at[:, pl.ds(head_start(head_col(q)), CHUNK)], slot)

        @pl.when(last & (q < 4))
        def _():
            load(w_proj.at[rows_at(lax.rem(q, 2)), cols(q // 2)], slot)

        @pl.when(last & (q >= 4) & (q < 12))
        def _():
            load(u_one.at[:, cols(q - 4)], slot)

        @pl.when(last & (q >= 12) & (q < 20))
        def _():
            load(u_two.at[rows_at(lax.rem(q - 12, 4)), cols((q - 12) // 4)], slot)

    def remote(src, dst, send, recv, to_dp, to_pp):
        return pltpu.make_async_remote_copy(
            src_ref=src, dst_ref=dst, send_sem=send, recv_sem=recv, device_id=(to_dp, to_pp), device_id_type=MESH
        )

    for c in range(8):
        load(up_chunk(c), c // 2 if c % 2 == 0 else 8 + (c // 2))
    for c in range(4):
        load(down_chunk(c // 2, 2 * (c % 2)), 4 + c)

    barrier = pltpu.get_barrier_semaphore()
    for o in range(1, n_dev):
        peer = lax.rem(me + o, n_dev)
        pl.semaphore_signal(barrier, inc=1, device_id=(peer // n_roles, lax.rem(peer, n_roles)), device_id_type=MESH)
    pl.semaphore_wait(barrier, n_dev - 1)

    def exchange(mb):
        return remote(rows.at[2 + mb], x_in.at[mb], ex_s.at[mb], ex_r.at[mb], 1 - dp, 0)

    def local_rows(mb):
        return pltpu.make_async_copy(rows.at[mb], x_out.at[mb], loc_sem.at[mb])

    @pl.when(role == 0)
    def _():
        for mb in range(2):
            exchange(mb).start()
        for mb in range(2):
            local_rows(mb).start()

    def piece(ref, mb, g):
        return ref.at[mb, body_rows, cols(g)]

    def hand_on(mb, g):
        i = 2 * mb + g
        return remote(piece(x_out, mb, g), piece(x_in, mb, g), xs_sem.at[i], xr_sem.at[i], dp, jnp.minimum(role + 1, last_role))

    def h_to_one(mb, g):
        i = 2 * mb + g
        return remote(piece(x_out, mb, g), piece(h_buf, mb, g), hs_sem.at[i], hr_sem.at[i], dp, 1)

    def h_to_two(mb, g):
        i = 2 * mb + g
        return remote(piece(x_out, mb, g), piece(h_buf, mb, g), hs2_sem.at[i], hr_sem.at[i], dp, 2)

    def h_relay(mb, g):
        i = 2 * mb + g
        return remote(piece(h_buf, mb, g), piece(h_buf, mb, g), rl_sem.at[i], hr_sem.at[i], dp, 0)

    def e_on(mb):
        return remote(x_in.at[mb], e_buf.at[mb], es_sem.at[mb], er_sem.at[mb], dp, last_role)

    def stage_pass(mb, carry):
        @pl.when(role == 0)
        def _():
            local_rows(mb).wait()
            exchange(mb).wait_recv()
            for r in range(0, x_in.shape[1], 8):
                at = pl.ds(r, 8)
                x_in[mb, at, :] = x_in[mb, at, :] + x_out[mb, at, :]

        @pl.when(role > 0)
        def _():
            for g in range(2):
                hand_on(mb, g).wait_recv()

        norm_into(xn, x_in.at[mb, body_rows])

        @pl.when(role == 0)
        def _():
            e_on(mb).start()

        def up(i, c2):
            @pl.when(mb == 0)
            def _():
                wait_slot(i)

            wait_slot(8 + i)
            for e, slot in ((0, i), (1, 8 + i)):
                for n in range(0, CHUNK, HALF):
                    y = dot(xn[...], wbuf[slot, :, pl.ds(n, HALF)])
                    at = pl.multiple_of((2 * i + e) * CHUNK + n, HALF)
                    hid[pl.ds(0, n_half), pl.ds(at, HALF)] = gelu(y)
            g2 = i // 2
            load(down_chunk(g2, 2 * lax.rem(i, 2) + 1), 8 + i)

            @pl.when(mb == 1)
            def _():
                issue_post(i)

            return c2

        lax.fori_loop(0, 4, up, 0)

        def down(g, c2):
            @pl.when(mb == 0)
            def _():
                wait_slot(4 + 2 * g)
                wait_slot(5 + 2 * g)

            wait_slot(8 + 2 * g)
            wait_slot(9 + 2 * g)
            slots = (4 + 2 * g, 8 + 2 * g, 5 + 2 * g, 9 + 2 * g)
            for n in range(0, CHUNK, HALF):
                y = None
                for k in range(4):
                    part = dot(hid[pl.ds(0, n_half), pl.ds(k * width, width)], wbuf[slots[k], :, pl.ds(n, HALF)])
                    y = part if y is None else y + part
                at = pl.ds(pl.multiple_of(g * CHUNK + n, HALF), HALF)
                x_out[mb, body_rows, at] = (x_in[mb, body_rows, at].astype(jnp.float32) + y).astype(jnp.bfloat16)

            @pl.when(mb == 0)
            def _():
                load(up_chunk(4 * g + 1), 8 + 2 * g)
                load(up_chunk(4 * g + 3), 9 + 2 * g)

            @pl.when(mb == 1)
            def _():
                issue_post(4 + 2 * g)
                issue_post(5 + 2 * g)
                issue_post(8 + 2 * g)
                issue_post(9 + 2 * g)

            @pl.when((role == 0) & (g == 1))
            def _():
                e_on(mb).wait_send()

            @pl.when(role < last_role)
            def _():
                hand_on(mb, g).start()

            @pl.when(last)
            def _():
                h_to_one(mb, g).start()
                h_to_two(mb, g).start()

            return c2

        lax.fori_loop(0, 2, down, 0)
        return carry

    lax.fori_loop(0, 2, stage_pass, 0)

    def z_piece(g):
        return z_buf.at[:, body_rows, cols(g)]

    def z_to_one(g):
        return remote(z_piece(g), z_piece(g), zs_sem.at[g], zr_sem.at[g], dp, 1)

    def z_to_two(g):
        return remote(z_piece(g), z_piece(g), zs2_sem.at[g], zr_sem.at[g], dp, 2)

    def z_relay(g):
        return remote(z_piece(g), z_piece(g), zl_sem.at[g], zr_sem.at[g], dp, 0)

    @pl.when(role < last_role)
    def _():
        for mb in range(2):
            for g in range(2):
                h_to_one(mb, g).wait_recv()

                @pl.when(role == 1)
                def _():
                    h_relay(mb, g).start()

        for mb in range(2):
            norm_into(n_buf.at[0, pl.ds(mb * n_half, n_half)], h_buf.at[mb], gain_f)

    @pl.when(last)
    def _():
        for mb in range(2):
            part = pl.ds(mb * n_half, n_half)
            norm_into(n_buf.at[0, part], x_out.at[mb, body_rows], gain_h)
            e_on(mb).wait_recv()
            shape = (n_half, e_buf.shape[1])
            shifted = lax.broadcasted_iota(jnp.int32, shape, 1) == lax.broadcasted_iota(jnp.int32, shape, 0) + 1
            hot = jnp.where(shifted, 1.0, 0.0).astype(jnp.bfloat16)
            for n in range(0, width, HALF):
                n_buf[1, part, pl.ds(n, HALF)] = dot(hot, e_buf[mb, :, pl.ds(n, HALF)]).astype(jnp.bfloat16)
            norm_into(n_buf.at[1, part], n_buf.at[1, part], gain_e)

        def proj(g, c2):
            wait_slot(2 * g)
            wait_slot(2 * g + 1)
            for n in range(0, CHUNK, HALF):
                y = dot(n_buf[0], wbuf[2 * g, :, pl.ds(n, HALF)]) + dot(n_buf[1], wbuf[2 * g + 1, :, pl.ds(n, HALF)])
                at = pl.ds(pl.multiple_of(g * CHUNK + n, HALF), HALF)
                for mb in range(2):
                    z_buf[mb, body_rows, at] = y[mb * n_half : (mb + 1) * n_half].astype(jnp.bfloat16)
            issue_post(12 + 2 * g)
            issue_post(13 + 2 * g)
            return c2

        lax.fori_loop(0, 2, proj, 0)
        for mb in range(2):
            norm_into(n_buf.at[0, pl.ds(mb * n_half, n_half)], z_buf.at[mb, body_rows], gain_m)

        def up(i, c2):
            wait_slot(4 + i)
            for n in range(0, CHUNK, HALF):
                y = dot(n_buf[0], wbuf[4 + i, :, pl.ds(n, HALF)])
                hid[:, pl.ds(pl.multiple_of(i * CHUNK + n, HALF), HALF)] = gelu(y)
            issue_post(16 + i)
            return c2

        lax.fori_loop(0, 8, up, 0)

        def down(g, c2):
            for k in range(4):
                wait_slot(4 * g + k)
            for n in range(0, CHUNK, HALF):
                y = None
                for k in range(4):
                    part = dot(hid[:, pl.ds(k * width, width)], wbuf[4 * g + k, :, pl.ds(n, HALF)])
                    y = part if y is None else y + part
                at = pl.ds(pl.multiple_of(g * CHUNK + n, HALF), HALF)
                for mb in range(2):
                    part = y[mb * n_half : (mb + 1) * n_half]
                    z_buf[mb, body_rows, at] = (z_buf[mb, body_rows, at].astype(jnp.float32) + part).astype(jnp.bfloat16)
            for k in range(4):
                issue_post(24 + 4 * g + k)
            z_to_one(g).start()
            z_to_two(g).start()
            return c2

        lax.fori_loop(0, 2, down, 0)

    top[...] = jnp.full(top.shape, NEG, jnp.float32)
    total[...] = jnp.zeros(total.shape, jnp.float32)
    pick[...] = jnp.zeros(pick.shape, jnp.float32)
    lane = lax.broadcasted_iota(jnp.int32, (n_rows, LANES), 1)

    def head(which):
        def step(q, c2):
            slot = lax.rem(q, N_SLOTS)
            wait_slot(slot)
            col = head_col(q)
            low = col * CHUNK
            first = head_start(col)
            for n in range(0, CHUNK, HALF):
                y = dot(n_buf[which], wbuf[slot, :, pl.ds(n, HALF)])
                skip = low - (first + n)
                rel = tgt[which] - (first + n)
                rel = jnp.where(rel >= skip, rel, -1)
                old = top[which]
                picked = pick[which]
                parts = []
                for c in range(0, HALF, LANES):
                    part = jnp.where(lane >= skip - c, y[:, c : c + LANES], NEG)
                    picked = picked + jnp.where(lane == rel - c, part, 0.0)
                    parts.append(part)
                new = functools.reduce(jnp.maximum, parts, old)
                acc = total[which] * jnp.exp(old - new)
                for part in parts:
                    acc = acc + jnp.exp(part - new)
                top[which] = new
                total[which] = acc
                pick[which] = picked
            issue_post(q + N_SLOTS)
            return c2

        return step

    lax.fori_loop(0, n_main, head(0), 0)

    @pl.when(role < last_role)
    def _():
        for g in range(2):
            z_to_one(g).wait_recv()

            @pl.when(role == 1)
            def _():
                z_relay(g).start()

    for mb in range(2):
        norm_into(n_buf.at[1, pl.ds(mb * n_half, n_half)], z_buf.at[mb, body_rows], gain_f)
    lax.fori_loop(q_mtp, q_end, head(1), 0)

    for which in range(2):
        m = top[which]
        row_m = jnp.max(m, axis=1, keepdims=True)
        row_s = jnp.sum(total[which] * jnp.exp(m - row_m), axis=1, keepdims=True)
        row_p = jnp.sum(pick[which], axis=1, keepdims=True)
        packed = jnp.where(lane == 0, row_m, jnp.where(lane == 1, row_s, jnp.where(lane == 2, row_p, 0.0)))
        stat[me, which] = packed.T[:8]

    def stats_to(o):
        peer = lax.rem(me + o, n_dev)
        return remote(stat.at[me], stat.at[me], ss_sem.at[o], sr_sem.at[o], peer // n_roles, lax.rem(peer, n_roles))

    def stats_from(o):
        source = lax.rem(me + n_dev - o, n_dev)
        return remote(stat.at[me], stat.at[source], ss_sem.at[o], sr_sem.at[o], dp, role)

    for o in range(1, n_dev):
        stats_to(o).start()

    @pl.when(role == 0)
    def _():
        for mb in range(2):
            exchange(mb).wait_send()

    for mb in range(2):
        for g in range(2):

            @pl.when(role < last_role)
            def _():
                hand_on(mb, g).wait_send()

            @pl.when(last)
            def _():
                h_to_one(mb, g).wait_send()
                h_to_two(mb, g).wait_send()

            @pl.when(role == 1)
            def _():
                h_relay(mb, g).wait_send()

    for g in range(2):

        @pl.when(last)
        def _():
            z_to_one(g).wait_send()
            z_to_two(g).wait_send()

        @pl.when(role == 1)
        def _():
            z_relay(g).wait_send()

    for o in range(1, n_dev):
        stats_from(o).wait_recv()
    for o in range(1, n_dev):
        stats_to(o).wait_send()

    def nll(data, which):
        s = [stat[data * n_roles + r, which] for r in range(n_roles)]
        m = functools.reduce(jnp.maximum, [v[0:1] for v in s])
        t = sum(v[1:2] * jnp.exp(v[0:1] - m) for v in s)
        return m + jnp.log(t) - sum(v[2:3] for v in s)

    n_all = n_data * n_rows
    loss = jnp.zeros((1, 1), jnp.float32)
    for data in range(n_data):
        loss = loss + jnp.sum(nll(data, 0), axis=1, keepdims=True) + MTP_WEIGHT * jnp.sum(nll(data, 1), axis=1, keepdims=True)
    out[0:1] = nll(dp, 0)
    out[1:2] = nll(dp, 1)
    out[2:3] = jnp.broadcast_to(loss / n_all, (1, n_rows))
    out[3:8] = jnp.zeros((5, n_rows), jnp.float32)


def run_mega(rows, tgt, gains, weights):
    n_ext, width = rows.shape[1], rows.shape[2]
    n_rows = tgt.shape[1]
    n_half = n_rows // 2
    ffn = weights[0].shape[3]
    bf16, f32 = jnp.bfloat16, jnp.float32
    vmem = pl.BlockSpec(memory_space=pltpu.VMEM)
    anywhere = pl.BlockSpec(memory_space=pl.ANY)
    dma = pltpu.SemaphoreType.DMA
    return pl.pallas_call(
        mega_kernel,
        in_specs=[anywhere, vmem, vmem, vmem, vmem, vmem] + [anywhere] * 6,
        out_specs=vmem,
        out_shape=jax.ShapeDtypeStruct((8, n_rows), f32),
        scratch_shapes=[
            pltpu.VMEM((N_SLOTS, width, CHUNK), bf16),
            pltpu.VMEM((2, n_ext, width), bf16),
            pltpu.VMEM((n_rows, ffn), bf16),
            pltpu.VMEM((2, n_ext, width), bf16),
            pltpu.VMEM((2, n_half, width), bf16),
            pltpu.VMEM((2, n_ext, width), bf16),
            pltpu.VMEM((2, n_rows, width), bf16),
            pltpu.VMEM((2, n_rows, LANES), f32),
            pltpu.VMEM((2, n_rows, LANES), f32),
            pltpu.VMEM((2, n_rows, LANES), f32),
            pltpu.VMEM((8, 2, 8, n_rows), f32),
            dma((N_SLOTS,)),
            dma((2,)), dma((4,)), dma((4,)), dma((2,)), dma((2,)), dma((2,)), dma((2,)),
            dma((4,)), dma((4,)), dma((4,)), dma((4,)),
            dma((2,)), dma((2,)), dma((2,)), dma((2,)),
            dma((8,)), dma((8,)),
        ],
        compiler_params=pltpu.CompilerParams(collective_id=0, has_side_effects=True, vmem_limit_bytes=67043328),
        name="mega",
    )(rows, tgt, *gains, *weights)


def solution(mesh):
    n_data = mesh.shape['dp']
    swap = [(i, (i + 1) % n_data) for i in range(n_data)]

    def body(tok_ids, emb_s, w_one, w_two, gain_f, gain_h, gain_e, gain_m, w_proj, u_one, u_two, w_out):
        role = lax.axis_index('pp')
        dp = lax.axis_index('dp')
        n_micro, batch_dev, seq_plus = tok_ids.shape
        seq_len = seq_plus - 2
        n_seq = n_micro * batch_dev
        table = emb_s[0]
        shard_rows = table.shape[0]
        seqs = tok_ids.reshape(n_seq, seq_plus)
        ids_mine = seqs[:, : seq_len + 1]
        ids_other = lax.ppermute(ids_mine, 'dp', swap)
        ids = jnp.concatenate([ids_mine, ids_other]) - dp * shard_rows
        owned = (ids >= 0) & (ids < shard_rows)
        rows = gather_rows(role, jnp.clip(ids, 0, shard_rows - 1), owned, table)
        targets = jnp.stack([seqs[:, 1 : seq_len + 1].reshape(-1), seqs[:, 2:].reshape(-1)])
        tgt = jnp.broadcast_to(targets[:, :, None], targets.shape + (LANES,))
        gains = [gain_f, gain_h, gain_e, gain_m]
        out = run_mega(rows, tgt, gains, [w_one, w_two, w_proj, u_one, u_two, w_out])
        main_nll = out[0].reshape(n_micro, batch_dev, seq_len)
        mtp_nll = out[1].reshape(n_micro, batch_dev, seq_len)
        return out[2, 0], main_nll, mtp_nll

    replicated = P()
    in_specs = (P(None, 'dp', None), P('pp', 'dp', None), P('pp'), P('pp'), replicated, replicated, replicated, replicated, replicated, replicated, replicated, replicated)
    out_specs = (replicated, P(None, 'dp', None), P(None, 'dp', None))
    return jax.shard_map(body, mesh=mesh, in_specs=in_specs, out_specs=out_specs, check_vma=False)
```

time: 3020 us -> 179 us (0.06)
  waiting for transfers between devices: 2330 us -> 1.47 us
  starting transfers between devices: 250 us -> 3.37 us
  blocking collectives: 221 us -> 0 us
  Pallas kernels: 0 us -> 167 us
  matrix products: 126 us -> 0 us
  local copies, waits for them, and re-layouts: 57.9 us -> 5.71 us
    all_gather x1 -> x0, waiting for transfers between devices: 2330 us -> none  [body(): table = lax.all_gather(emb_s[0], 'dp', axis=0, tiled=True)]
    ppermute x10 -> x1, starting transfers between devices: 250 us -> 3.37 us  [body(): ids_other = lax.ppermute(ids_mine, 'dp', swap)]
    psum x2 -> x0, blocking collectives: 221 us -> none  [the longest x1 216 us: body(): lax.psum(main_all[n_stages - 1:], 'pp').reshape(n_micro, batch_dev, seq_len)]
    pallas_call x0 -> x2, Pallas kernels: none -> 167 us  [the longest x1 153 us: run_mega(): pl.pallas_call(mega_kernel, in_specs=[anywhere, vmem, vmem, vmem, vmem, v...]
    dot_general x5 -> x0, matrix products: 126 us -> none  [mlp_add(): jnp.dot(hidden, w_down, preferred_element_type=jnp.float32)]
  transfers between devices with their start and end apart: 11 -> 1, of which waited for: 1 -> 1; matrix products, arithmetic and copies ran while one was open for 5% -> 0% of each run, Pallas kernels for 0% -> 0%
where the time goes in v1:
time: 179 us
  Pallas kernels  167 us (93%)
  local copies, waits for them, and re-layouts  5.71 us (3%)
  starting transfers between devices  3.37 us (2%)
    pallas_call x1, Pallas kernels, run_mega(): pl.pallas_call(mega_kernel, in_specs=[anywhere, vmem, vmem, vmem, vmem, v...  153 us
    pallas_call x1, Pallas kernels, gather_rows(): pl.pallas_call(functools.partial(gather_kernel, n_ids), grid_spec=pltpu.P...  14.1 us
  transfers between devices with their start and end apart: 1, of which 1 were waited for; matrix products, arithmetic and copies ran while one was open for 0% of the time, Pallas kernels for 0%

profile of v1, /device:TPU:0, one launch (start us, length us, event | category | flops | bytes accessed | tf_op | source)
XLA Modules:
  0.0 178.8 jit_solution(17201970603448590117)
XLA Ops:
  0.6 0.7 copy.22
  1.3 3.4 %collective-permute-start = (s32[2,129]{1,0:T(2,128)S(1)}, s32[2,129]{1,0:T(2,128)S(1)}, u32[]{:S(2)}, u32[]{:S(2)}) collective-permute-start(s32[2,129]{1,0:T(2,128)S(1)} %bitcast.19), channel_id=1, source_target_pairs={{0,4},{4,0},{1,5},{5,1},{2,6},{6,2},{3,7},{7,3}} | collective-permute-start | bytes 3104 | tf_op jit(solution)/shard_map/ppermute | solution.py:564
  4.7 0.1 fusion.9
  4.8 1.5 collective-permute-done
  6.3 0.2 copy.17.sel_ref
  6.4 0.1 min.12
  6.5 14.1 %gather_rows.1.rows = bf16[4,136,2048]{2,1,0:T(8,128)(2,1)S(1)} custom-call(s32[1]{0:T(128)} %bitcast.flag_ref, s32[516]{0:T(1024)S(1)} %add_select_fusion.1.grp_ref, s32[4,136,1]{2,1,0:T(8,128)S(1)} %copy.17.sel_ref, bf16[25152,2048]{1,0:T(8,128)(2,1)} %bitcast.2.table_ref), custom_call_target="tpu_custom_call" | custom-call | tf_op jit(solution)/shard_map/gather_rows/pallas_call | solution.py:54
  20.7 0.0 copy-start
  20.7 1.4 copy-done
  22.1 0.8 broadcast_in_dim.7.tgt
  22.9 153.3 %mega.1 = f32[8,256]{1,0:T(8,128)} custom-call(bf16[4,136,2048]{2,1,0:T(8,128)(2,1)} %copy-done, s32[2,256,128]{2,1,0:T(8,128)} %broadcast_in_dim.7.tgt, bf16[2048]{0:T(1024)(128)(2,1)} %gain_f.1, bf16[2048]{0:T(1024)(128)(2,1)} %gain_h.1, bf16[2048]{0:T(1024)(128)(2,1)} %gain_e.1, bf16[2048]{0:T(1024)(128)(2,1)} %gain_m.1, ...), custom_call_target="tpu_custom_call" | custom-call | tf_op jit(solution)/shard_map/mega/pallas_call | solution.py:522
  176.2 1.3 slice_bitcast_fusion
  177.6 1.2 slice.21
  (5 shorter events, 0.1 us)
Async XLA Ops:
  1.3 4.9 %collective-permute-start = (s32[2,129]{1,0:T(2,128)S(1)}, s32[2,129]{1,0:T(2,128)S(1)}, u32[]{:S(2)}, u32[]{:S(2)}) collective-permute-start(s32[2,129]{1,0:T(2,128)S(1)} %bitcast.19), channel_id=1, source_target_pairs={{0,4},{4,0},{1,5},{5,1},{2,6},{6,2},{3,7},{7,3}} | collective-permute-start | bytes 3104 | tf_op jit(solution)/shard_map/ppermute | solution.py:564
  20.7 1.4 copy-start

commit v2 on v1

--- a/solution.py
+++ b/solution.py
@@ -16,31 +16,53 @@
 N_SLOTS = 12
 MESH = pl.DeviceIdType.MESH
 GROUP = 8
-
-
-def gather_kernel(n_ids, flag_ref, grp_ref, sel_ref, table_ref, out_ref, buf, sems):
+MAIN_SHARE = 32
+MTP_SHARE = 24
+
+
+def gather_kernel(n_ids, flag_ref, grp_ref, count_ref, sel_ref, table_ref, out_ref, buf, rows, sems, out_sems):
     n_batches = buf.shape[0]
 
     def start(batch):
         def one(j, carry):
-            first = pl.multiple_of(grp_ref[batch * n_ids + j] * GROUP, GROUP)
-            pltpu.make_async_copy(
-                table_ref.at[pl.ds(first, GROUP), :], buf.at[batch, j], sems.at[batch]
-            ).start()
+            grp = grp_ref[batch * n_ids + j]
+
+            @pl.when(grp >= 0)
+            def _():
+                first = pl.multiple_of(grp * GROUP, GROUP)
+                pltpu.make_async_copy(
+                    table_ref.at[pl.ds(first, GROUP), :], buf.at[batch, j], sems.at[batch]
+                ).start()
+
             return carry
 
         lax.fori_loop(0, n_ids, one, 0, unroll=43)
 
+    def wait(batch):
+        def one(j, carry):
+            pltpu.make_async_copy(buf.at[batch, 0], buf.at[batch, 0], sems.at[batch]).wait()
+            return carry
+
+        lax.fori_loop(0, count_ref[batch], one, 0)
+
     @pl.when(flag_ref[0] == 0)
     def _():
         for batch in range(n_batches):
+            def clear(j, carry):
+                buf[batch, j] = jnp.zeros(buf.shape[2:], buf.dtype)
+                return carry
+
+            lax.fori_loop(0, n_ids, clear, 0, unroll=3)
             start(batch)
         col = lax.broadcasted_iota(jnp.int32, (out_ref.shape[1], n_ids * GROUP), 1)
         for batch in range(n_batches):
-            pltpu.make_async_copy(buf.at[batch], buf.at[batch], sems.at[batch]).wait()
+            wait(batch)
             hot = jnp.where(col == sel_ref[batch], 1.0, 0.0).astype(jnp.bfloat16)
-            rows = buf[batch].reshape(n_ids * GROUP, -1)
-            out_ref[batch] = jnp.dot(hot, rows, preferred_element_type=jnp.float32).astype(jnp.bfloat16)
+            src = buf[batch].reshape(n_ids * GROUP, -1)
+            rows[batch] = jnp.dot(hot, src, preferred_element_type=jnp.float32).astype(jnp.bfloat16)
+            pltpu.make_async_copy(rows.at[batch], out_ref.at[batch], out_sems.at[batch]).start()
+        for batch in range(n_batches):
+            pltpu.make_async_copy(rows.at[batch], out_ref.at[batch], out_sems.at[batch]).wait()
 
 
 def gather_rows(flag, local, owned, table):
@@ -49,24 +71,30 @@
     width = table.shape[1]
     grp = local // GROUP
     sub = local - grp * GROUP
+    grp = jnp.where(owned, grp, -1)
     sel = jnp.where(owned, jnp.arange(n_ids, dtype=jnp.int32) * GROUP + sub, -1)
     sel = jnp.pad(sel, ((0, 0), (0, n_out - n_ids)), constant_values=-1)
     return pl.pallas_call(
         functools.partial(gather_kernel, n_ids),
         grid_spec=pltpu.PrefetchScalarGridSpec(
-            num_scalar_prefetch=2,
+            num_scalar_prefetch=3,
             grid=(),
             in_specs=[pl.BlockSpec(memory_space=pltpu.VMEM), pl.BlockSpec(memory_space=pl.ANY)],
-            out_specs=pl.BlockSpec(memory_space=pltpu.VMEM),
+            out_specs=pl.BlockSpec(memory_space=pltpu.HBM),
             scratch_shapes=[
                 pltpu.VMEM((n_batches, n_ids, GROUP, width), table.dtype),
+                pltpu.VMEM((n_batches, n_out, width), table.dtype),
+                pltpu.SemaphoreType.DMA((n_batches,)),
                 pltpu.SemaphoreType.DMA((n_batches,)),
             ],
         ),
         out_shape=jax.ShapeDtypeStruct((n_batches, n_out, width), table.dtype),
-        compiler_params=pltpu.CompilerParams(vmem_limit_bytes=40 << 20),
+        compiler_params=pltpu.CompilerParams(vmem_limit_bytes=66_000_000),
+        cost_estimate=pl.CostEstimate(
+            flops=2 * n_batches * n_out * n_ids * GROUP * width * 8, bytes_accessed=n_batches * n_ids * GROUP * width * 2, transcendentals=0
+        ),
         name="gather_rows",
-    )(flag.reshape(1), grp.reshape(-1), sel[..., None], table)
+    )(flag.reshape(1), grp.reshape(-1), jnp.sum(owned, axis=1, dtype=jnp.int32), sel[..., None], table)
 
 
 def scaled_rows(rows, gain):
@@ -94,8 +122,8 @@
 
 def mega_kernel(
     rows, tgt, gain_f, gain_h, gain_e, gain_m, w_one, w_two, w_proj, u_one, u_two, w_out,
-    out, wbuf, x_in, hid, x_out, h_buf, e_buf, n_buf, top, total, pick, stat,
-    wsem, loc_sem, xs_sem, xr_sem, ex_s, ex_r, es_sem, er_sem, hs_sem, hs2_sem, hr_sem, rl_sem, zs_sem, zs2_sem, zr_sem, zl_sem, ss_sem, sr_sem,
+    out, wbuf, x_in, hid, x_out, h_buf, n_buf, top, total, pick, stat,
+    wsem, loc_sem, xs_sem, xr_sem, ex_s, ex_r, es_sem, er_sem, hs_sem, hs2_sem, hr_sem, rl_sem, zs_sem, zs2_sem, zr_sem, zl_sem, zx_s, zx_r, hx_s, hx_r, el_sem, ss_sem, sr_sem,
 ):
     role = lax.axis_index('pp')
     dp = lax.axis_index('dp')
@@ -112,10 +140,19 @@
     z_buf = x_in
     last_role = n_roles - 1
     last = role == last_role
-    lane_main = jnp.where(role == 0, 0, jnp.where(role == 2, 1, 2))
-    n_main = jnp.where(last, 0, (n_cols - lane_main + 2) // 3)
-    n_mtp = (n_cols - role + 3) // 4
-    q_mtp = jnp.where(last, 20, n_main)
+    is_mtp = role >= n_roles - 2
+    own = jnp.maximum(role - (n_roles - 2), 0)
+    mate = jnp.where(role == last_role, last_role - 1, last_role)
+    large = (n_cols * MAIN_SHARE) // 100
+    small = (n_cols - 2 * large + 1) // 2
+    main_at = jnp.where(is_mtp, 2 * large + own * small, role * large)
+    n_main = jnp.where(is_mtp, jnp.where(last, n_cols - 2 * large - small, small), large)
+    few = (n_cols * MTP_SHARE) // 100
+    more = (n_cols - 2 * few + 1) // 2
+    mtp_at = jnp.where(is_mtp, 2 * few + own * more, role * few)
+    n_mtp = jnp.where(is_mtp, jnp.where(last, n_cols - 2 * few - more, more), few)
+    q_main = jnp.where(is_mtp, 10, 0)
+    q_mtp = q_main + n_main
     q_end = q_mtp + n_mtp
 
     def load(src, slot):
@@ -137,7 +174,7 @@
         return w_two.at[0, 0, rows_at(k), cols(g)]
 
     def head_col(q):
-        return jnp.where(q < n_main, lane_main + 3 * q, role + 4 * (q - q_mtp))
+        return jnp.where(q < q_mtp, main_at + q - q_main, mtp_at + q - q_mtp)
 
     def head_start(col):
         return pl.multiple_of(jnp.minimum(col * CHUNK, n_vocab - CHUNK), LANES)
@@ -145,21 +182,21 @@
     def issue_post(q):
         slot = lax.rem(q, N_SLOTS)
 
-        @pl.when(((q < n_main) | (q >= q_mtp)) & (q < q_end))
+        @pl.when((q >= q_main) & (q < q_end))
         def _():
             load(w_out.at[:, pl.ds(head_start(head_col(q)), CHUNK)], slot)
 
-        @pl.when(last & (q < 4))
+        @pl.when(is_mtp & (q < 2))
         def _():
-            load(w_proj.at[rows_at(lax.rem(q, 2)), cols(q // 2)], slot)
-
-        @pl.when(last & (q >= 4) & (q < 12))
+            load(w_proj.at[rows_at(q), cols(own)], slot)
+
+        @pl.when(is_mtp & (q >= 2) & (q < 6))
         def _():
-            load(u_one.at[:, cols(q - 4)], slot)
-
-        @pl.when(last & (q >= 12) & (q < 20))
+            load(u_one.at[:, cols(4 * own + q - 2)], slot)
+
+        @pl.when(is_mtp & (q >= 6) & (q < 10))
         def _():
-            load(u_two.at[rows_at(lax.rem(q - 12, 4)), cols((q - 12) // 4)], slot)
+            load(u_two.at[rows_at(q - 6), cols(own)], slot)
 
     def remote(src, dst, send, recv, to_dp, to_pp):
         return pltpu.make_async_remote_copy(
@@ -185,8 +222,7 @@
 
     @pl.when(role == 0)
     def _():
-        for mb in range(2):
-            exchange(mb).start()
+        exchange(0).start()
         for mb in range(2):
             local_rows(mb).start()
 
@@ -210,13 +246,37 @@
         return remote(piece(h_buf, mb, g), piece(h_buf, mb, g), rl_sem.at[i], hr_sem.at[i], dp, 0)
 
     def e_on(mb):
-        return remote(x_in.at[mb], e_buf.at[mb], es_sem.at[mb], er_sem.at[mb], dp, last_role)
+        return remote(x_in.at[mb], h_buf.at[mb], es_sem.at[mb], er_sem.at[mb], dp, last_role)
+
+    def half_rows(mb):
+        return pl.ds(mb * n_half, n_half)
+
+    def en_relay(mb):
+        part = n_buf.at[1, half_rows(mb)]
+        return remote(part, part, el_sem.at[mb], er_sem.at[mb], dp, last_role - 1)
+
+    @pl.when(last)
+    def _():
+        for mb in range(2):
+            e_on(mb).wait_recv()
+            shape = (n_half, h_buf.shape[1])
+            shifted = lax.broadcasted_iota(jnp.int32, shape, 1) == lax.broadcasted_iota(jnp.int32, shape, 0) + 1
+            hot = jnp.where(shifted, 1.0, 0.0).astype(jnp.bfloat16)
+            for n in range(0, width, HALF):
+                n_buf[1, half_rows(mb), pl.ds(n, HALF)] = dot(hot, h_buf[mb, :, pl.ds(n, HALF)]).astype(jnp.bfloat16)
+            norm_into(n_buf.at[1, half_rows(mb)], n_buf.at[1, half_rows(mb)], gain_e)
+            en_relay(mb).start()
 
     def stage_pass(mb, carry):
         @pl.when(role == 0)
         def _():
             local_rows(mb).wait()
             exchange(mb).wait_recv()
+
+            @pl.when(mb == 0)
+            def _():
+                exchange(1).start()
+
             for r in range(0, x_in.shape[1], 8):
                 at = pl.ds(r, 8)
                 x_in[mb, at, :] = x_in[mb, at, :] + x_out[mb, at, :]
@@ -303,17 +363,36 @@
 
     lax.fori_loop(0, 2, stage_pass, 0)
 
-    def z_piece(g):
-        return z_buf.at[:, body_rows, cols(g)]
-
-    def z_to_one(g):
-        return remote(z_piece(g), z_piece(g), zs_sem.at[g], zr_sem.at[g], dp, 1)
-
-    def z_to_two(g):
-        return remote(z_piece(g), z_piece(g), zs2_sem.at[g], zr_sem.at[g], dp, 2)
-
-    def z_relay(g):
-        return remote(z_piece(g), z_piece(g), zl_sem.at[g], zr_sem.at[g], dp, 0)
+    def z_half(g, n):
+        return z_buf.at[:, body_rows, pl.ds(pl.multiple_of(g * CHUNK + n * HALF, HALF), HALF)]
+
+    def z_to_one(g, n):
+        return remote(z_half(g, n), z_half(g, n), zs_sem.at[n], zr_sem.at[2 * g + n], dp, 1)
+
+    def z_to_peer(g, n):
+        return remote(z_half(g, n), z_half(g, n), zs2_sem.at[n], zr_sem.at[2 * g + n], dp, mate)
+
+    def z_relay(g, n):
+        return remote(z_half(g, n), z_half(g, n), zl_sem.at[2 * g + n], zr_sem.at[2 * g + n], dp, 0)
+
+    def zx(g):
+        piece_g = z_buf.at[:, body_rows, cols(g)]
+        return remote(piece_g, piece_g, zx_s.at[0], zx_r.at[0], dp, mate)
+
+    def hx(g, i):
+        piece_g = hid.at[:, cols(4 * g + i)]
+        return remote(piece_g, piece_g, hx_s.at[i], hx_r.at[i], dp, mate)
+
+    def norm_h(gain):
+        for mb in range(2):
+
+            @pl.when(last)
+            def _():
+                norm_into(n_buf.at[0, half_rows(mb)], x_out.at[mb, body_rows], gain)
+
+            @pl.when(role < last_role)
+            def _():
+                norm_into(n_buf.at[0, half_rows(mb)], h_buf.at[mb, body_rows], gain)
 
     @pl.when(role < last_role)
     def _():
@@ -325,67 +404,64 @@
                 def _():
                     h_relay(mb, g).start()
 
+    @pl.when(is_mtp)
+    def _():
         for mb in range(2):
-            norm_into(n_buf.at[0, pl.ds(mb * n_half, n_half)], h_buf.at[mb], gain_f)
-
-    @pl.when(last)
-    def _():
+
+            @pl.when(role < last_role)
+            def _():
+                en_relay(mb).wait_recv()
+
+            @pl.when(last)
+            def _():
+                en_relay(mb).wait_send()
+
+        norm_h(gain_h)
+
+        wait_slot(0)
+        wait_slot(1)
+        for n in range(0, CHUNK, HALF):
+            y = dot(n_buf[0], wbuf[0, :, pl.ds(n, HALF)]) + dot(n_buf[1], wbuf[1, :, pl.ds(n, HALF)])
+            at = pl.ds(pl.multiple_of(own * CHUNK + n, HALF), HALF)
+            for mb in range(2):
+                z_buf[mb, body_rows, at] = y[mb * n_half : (mb + 1) * n_half].astype(jnp.bfloat16)
+        issue_post(12)
+        issue_post(13)
+        zx(own).start()
+        zx(1 - own).wait_recv()
         for mb in range(2):
-            part = pl.ds(mb * n_half, n_half)
-            norm_into(n_buf.at[0, part], x_out.at[mb, body_rows], gain_h)
-            e_on(mb).wait_recv()
-            shape = (n_half, e_buf.shape[1])
-            shifted = lax.broadcasted_iota(jnp.int32, shape, 1) == lax.broadcasted_iota(jnp.int32, shape, 0) + 1
-            hot = jnp.where(shifted, 1.0, 0.0).astype(jnp.bfloat16)
-            for n in range(0, width, HALF):
-                n_buf[1, part, pl.ds(n, HALF)] = dot(hot, e_buf[mb, :, pl.ds(n, HALF)]).astype(jnp.bfloat16)
-            norm_into(n_buf.at[1, part], n_buf.at[1, part], gain_e)
-
-        def proj(g, c2):
-            wait_slot(2 * g)
-            wait_slot(2 * g + 1)
+            norm_into(n_buf.at[0, half_rows(mb)], z_buf.at[mb, body_rows], gain_m)
+
+        def up(i, c2):
+            wait_slot(2 + i)
             for n in range(0, CHUNK, HALF):
-                y = dot(n_buf[0], wbuf[2 * g, :, pl.ds(n, HALF)]) + dot(n_buf[1], wbuf[2 * g + 1, :, pl.ds(n, HALF)])
-                at = pl.ds(pl.multiple_of(g * CHUNK + n, HALF), HALF)
-                for mb in range(2):
-                    z_buf[mb, body_rows, at] = y[mb * n_half : (mb + 1) * n_half].astype(jnp.bfloat16)
-            issue_post(12 + 2 * g)
-            issue_post(13 + 2 * g)
+                y = dot(n_buf[0], wbuf[2 + i, :, pl.ds(n, HALF)])
+                hid[:, pl.ds(pl.multiple_of((4 * own + i) * CHUNK + n, HALF), HALF)] = gelu(y)
+            issue_post(14 + i)
+            hx(own, i).start()
             return c2
 
-        lax.fori_loop(0, 2, proj, 0)
-        for mb in range(2):
-            norm_into(n_buf.at[0, pl.ds(mb * n_half, n_half)], z_buf.at[mb, body_rows], gain_m)
-
-        def up(i, c2):
-            wait_slot(4 + i)
-            for n in range(0, CHUNK, HALF):
-                y = dot(n_buf[0], wbuf[4 + i, :, pl.ds(n, HALF)])
-                hid[:, pl.ds(pl.multiple_of(i * CHUNK + n, HALF), HALF)] = gelu(y)
-            issue_post(16 + i)
-            return c2
-
-        lax.fori_loop(0, 8, up, 0)
-
-        def down(g, c2):
+        lax.fori_loop(0, 4, up, 0)
+        zx(own).wait_send()
+        for i in range(4):
+            hx(1 - own, i).wait_recv()
+        for k in range(4):
+            wait_slot(6 + k)
+        for n in range(2):
+            y = None
             for k in range(4):
-                wait_slot(4 * g + k)
-            for n in range(0, CHUNK, HALF):
-                y = None
-                for k in range(4):
-                    part = dot(hid[:, pl.ds(k * width, width)], wbuf[4 * g + k, :, pl.ds(n, HALF)])
-                    y = part if y is None else y + part
-                at = pl.ds(pl.multiple_of(g * CHUNK + n, HALF), HALF)
-                for mb in range(2):
-                    part = y[mb * n_half : (mb + 1) * n_half]
-                    z_buf[mb, body_rows, at] = (z_buf[mb, body_rows, at].astype(jnp.float32) + part).astype(jnp.bfloat16)
-            for k in range(4):
-                issue_post(24 + 4 * g + k)
-            z_to_one(g).start()
-            z_to_two(g).start()
-            return c2
-
-        lax.fori_loop(0, 2, down, 0)
+                part = dot(hid[:, pl.ds(k * width, width)], wbuf[6 + k, :, pl.ds(n * HALF, HALF)])
+                y = part if y is None else y + part
+            at = pl.ds(pl.multiple_of(own * CHUNK + n * HALF, HALF), HALF)
+            for mb in range(2):
+                part = y[mb * n_half : (mb + 1) * n_half]
+                z_buf[mb, body_rows, at] = (z_buf[mb, body_rows, at].astype(jnp.float32) + part).astype(jnp.bfloat16)
+            z_to_one(own, n).start()
+            z_to_peer(own, n).start()
+        for k in range(4):
+            issue_post(18 + k)
+
+    norm_h(gain_f)
 
     top[...] = jnp.full(top.shape, NEG, jnp.float32)
     total[...] = jnp.zeros(total.shape, jnp.float32)
@@ -423,16 +499,22 @@
 
         return step
 
-    lax.fori_loop(0, n_main, head(0), 0)
-
-    @pl.when(role < last_role)
-    def _():
-        for g in range(2):
-            z_to_one(g).wait_recv()
-
-            @pl.when(role == 1)
-            def _():
-                z_relay(g).start()
+    lax.fori_loop(q_main, q_mtp, head(0), 0)
+
+    @pl.when(is_mtp)
+    def _():
+        for n in range(2):
+            z_to_peer(1 - own, n).wait_recv()
+
+    @pl.when(role < n_roles - 2)
+    def _():
+        for n in range(2):
+            for g in range(2):
+                z_to_one(g, n).wait_recv()
+
+                @pl.when(role == 1)
+                def _():
+                    z_relay(g, n).start()
 
     for mb in range(2):
         norm_into(n_buf.at[1, pl.ds(mb * n_half, n_half)], z_buf.at[mb, body_rows], gain_f)
@@ -478,16 +560,19 @@
             def _():
                 h_relay(mb, g).wait_send()
 
-    for g in range(2):
-
-        @pl.when(last)
-        def _():
-            z_to_one(g).wait_send()
-            z_to_two(g).wait_send()
-
-        @pl.when(role == 1)
-        def _():
-            z_relay(g).wait_send()
+    @pl.when(is_mtp)
+    def _():
+        for n in range(2):
+            z_to_one(own, n).wait_send()
+            z_to_peer(own, n).wait_send()
+        for i in range(4):
+            hx(own, i).wait_send()
+
+    @pl.when(role == 1)
+    def _():
+        for g in range(2):
+            for n in range(2):
+                z_relay(g, n).wait_send()
 
     for o in range(1, n_dev):
         stats_from(o).wait_recv()
@@ -529,7 +614,6 @@
             pltpu.VMEM((2, n_ext, width), bf16),
             pltpu.VMEM((n_rows, ffn), bf16),
             pltpu.VMEM((2, n_ext, width), bf16),
-            pltpu.VMEM((2, n_half, width), bf16),
             pltpu.VMEM((2, n_ext, width), bf16),
             pltpu.VMEM((2, n_rows, width), bf16),
             pltpu.VMEM((2, n_rows, LANES), f32),
@@ -539,7 +623,8 @@
             dma((N_SLOTS,)),
             dma((2,)), dma((4,)), dma((4,)), dma((2,)), dma((2,)), dma((2,)), dma((2,)),
             dma((4,)), dma((4,)), dma((4,)), dma((4,)),
-            dma((2,)), dma((2,)), dma((2,)), dma((2,)),
+            dma((2,)), dma((2,)), dma((4,)), dma((4,)),
+            dma((1,)), dma((1,)), dma((4,)), dma((4,)), dma((2,)),
             dma((8,)), dma((8,)),
         ],
         compiler_params=pltpu.CompilerParams(collective_id=0, has_side_effects=True, vmem_limit_bytes=67043328),
@@ -562,9 +647,9 @@
         seqs = tok_ids.reshape(n_seq, seq_plus)
         ids_mine = seqs[:, : seq_len + 1]
         ids_other = lax.ppermute(ids_mine, 'dp', swap)
-        ids = jnp.concatenate([ids_mine, ids_other]) - dp * shard_rows
-        owned = (ids >= 0) & (ids < shard_rows)
-        rows = gather_rows(role, jnp.clip(ids, 0, shard_rows - 1), owned, table)
+
+        local = jnp.concatenate([ids_mine, ids_other]) - dp * shard_rows
+        rows = gather_rows(role, jnp.clip(local, 0, shard_rows - 1), (local >= 0) & (local < shard_rows), table)
         targets = jnp.stack([seqs[:, 1 : seq_len + 1].reshape(-1), seqs[:, 2:].reshape(-1)])
         tgt = jnp.broadcast_to(targets[:, :, None], targets.shape + (LANES,))
         gains = [gain_f, gain_h, gain_e, gain_m]

time: 179 us -> 173 us (0.966)
  Pallas kernels: 167 us -> 160 us
    pallas_call x1, Pallas kernels: 153 us -> 149 us  [run_mega(): pl.pallas_call(mega_kernel, in_specs=[anywhere, vmem, vmem, vmem, vmem, v...]
    pallas_call x1, Pallas kernels: 14.1 us -> 11 us  [gather_rows(): pl.pallas_call(functools.partial(gather_kernel, n_ids), grid_spec=pltpu.P...]
where the time goes in v2:
time: 173 us; the launch traced here: 172 us
  Pallas kernels  160 us (92%)
  local copies, waits for them, and re-layouts  5.16 us (3%)
  starting transfers between devices  3.37 us (2%)
    pallas_call x1, Pallas kernels, run_mega(): pl.pallas_call(mega_kernel, in_specs=[anywhere, vmem, vmem, vmem, vmem, v...  149 us
    pallas_call x1, Pallas kernels, gather_rows(): pl.pallas_call(functools.partial(gather_kernel, n_ids), grid_spec=pltpu.P...  11 us
  transfers between devices with their start and end apart: 1, of which 1 were waited for; matrix products, arithmetic and copies ran while one was open for 0% of the time, Pallas kernels for 0%

profile of v2, /device:TPU:0, one launch (start us, length us, event | category | flops | bytes accessed | tf_op | source)
XLA Modules:
  0.0 172.4 jit_solution(18298384120794163264)
XLA Ops:
  0.6 0.7 copy.22
  1.3 3.4 %collective-permute-start = (s32[2,129]{1,0:T(2,128)S(1)}, s32[2,129]{1,0:T(2,128)S(1)}, u32[]{:S(2)}, u32[]{:S(2)}) collective-permute-start(s32[2,129]{1,0:T(2,128)S(1)} %bitcast.19), channel_id=1, source_target_pairs={{0,4},{4,0},{1,5},{5,1},{2,6},{6,2},{3,7},{7,3}} | collective-permute-start | bytes 3104 | tf_op jit(solution)/shard_map/ppermute | solution.py:649
  4.7 0.1 fusion.11
  4.8 1.5 collective-permute-done
  6.3 0.1 and.19
  6.4 0.6 convert_reduce_fusion.count_ref
  7.0 0.1 min.12
  7.1 0.9 copy.17.sel_ref
  8.0 0.6 fusion.1.grp_ref
  8.5 11.0 %gather_rows.1.rows = bf16[4,136,2048]{2,1,0:T(8,128)(2,1)} custom-call(s32[1]{0:T(128)} %bitcast.flag_ref, s32[516]{0:T(1024)} %fusion.1.grp_ref, s32[4]{0:T(128)} %convert_reduce_fusion.count_ref, s32[4,136,1]{2,1,0:T(8,128)} %copy.17.sel_ref, bf16[25152,2048]{1,0:T(8,128)(2,1)} %bitcast.2.table_ref), custom_call_target="tpu_custom_call" | custom-call | flops 18396217344 | bytes 16908288 | tf_op jit(solution)/shard_map/gather_rows/pallas_call | solution.py:77
  19.6 0.8 broadcast_in_dim.14.tgt
  20.4 149.5 %mega.1 = f32[8,256]{1,0:T(8,128)} custom-call(bf16[4,136,2048]{2,1,0:T(8,128)(2,1)} %gather_rows.1.rows, s32[2,256,128]{2,1,0:T(8,128)} %broadcast_in_dim.14.tgt, bf16[2048]{0:T(1024)(128)(2,1)} %gain_f.1, bf16[2048]{0:T(1024)(128)(2,1)} %gain_h.1, bf16[2048]{0:T(1024)(128)(2,1)} %gain_e.1, bf16[2048]{0:T(1024)(128)(2,1)} %gain_m.1, ...), custom_call_target="tpu_custom_call" | custom-call | tf_op jit(solution)/shard_map/mega/pallas_call | solution.py:607
  169.9 1.3 slice_bitcast_fusion
  171.2 1.2 slice.21
  (4 shorter events, 0.0 us)
Async XLA Ops:
  1.3 4.9 %collective-permute-start = (s32[2,129]{1,0:T(2,128)S(1)}, s32[2,129]{1,0:T(2,128)S(1)}, u32[]{:S(2)}, u32[]{:S(2)}) collective-permute-start(s32[2,129]{1,0:T(2,128)S(1)} %bitcast.19), channel_id=1, source_target_pairs={{0,4},{4,0},{1,5},{5,1},{2,6},{6,2},{3,7},{7,3}} | collective-permute-start | bytes 3104 | tf_op jit(solution)/shard_map/ppermute | solution.py:649

commit v3 on v2

--- a/solution.py
+++ b/solution.py
@@ -203,10 +203,11 @@
             src_ref=src, dst_ref=dst, send_sem=send, recv_sem=recv, device_id=(to_dp, to_pp), device_id_type=MESH
         )
 
-    for c in range(8):
-        load(up_chunk(c), c // 2 if c % 2 == 0 else 8 + (c // 2))
-    for c in range(4):
-        load(down_chunk(c // 2, 2 * (c % 2)), 4 + c)
+    def first_loads(chunks):
+        for c in chunks:
+            load(up_chunk(c), c // 2 if c % 2 == 0 else 8 + (c // 2))
+
+    first_loads(range(2))
 
     barrier = pltpu.get_barrier_semaphore()
     for o in range(1, n_dev):
@@ -222,9 +223,14 @@
 
     @pl.when(role == 0)
     def _():
-        exchange(0).start()
+        for mb in range(2):
+            exchange(mb).start()
         for mb in range(2):
             local_rows(mb).start()
+
+    first_loads(range(2, 8))
+    for c in range(4):
+        load(down_chunk(c // 2, 2 * (c % 2)), 4 + c)
 
     def piece(ref, mb, g):
         return ref.at[mb, body_rows, cols(g)]
@@ -272,11 +278,6 @@
         def _():
             local_rows(mb).wait()
             exchange(mb).wait_recv()
-
-            @pl.when(mb == 0)
-            def _():
-                exchange(1).start()
-
             for r in range(0, x_in.shape[1], 8):
                 at = pl.ds(r, 8)
                 x_in[mb, at, :] = x_in[mb, at, :] + x_out[mb, at, :]
@@ -305,11 +306,6 @@
                     hid[pl.ds(0, n_half), pl.ds(at, HALF)] = gelu(y)
             g2 = i // 2
             load(down_chunk(g2, 2 * lax.rem(i, 2) + 1), 8 + i)
-
-            @pl.when(mb == 1)
-            def _():
-                issue_post(i)
-
             return c2
 
         lax.fori_loop(0, 4, up, 0)
@@ -338,6 +334,8 @@
 
             @pl.when(mb == 1)
             def _():
+                issue_post(2 * g)
+                issue_post(2 * g + 1)
                 issue_post(4 + 2 * g)
                 issue_post(5 + 2 * g)
                 issue_post(8 + 2 * g)

time: 173 us -> 161 us (0.931)
  Pallas kernels: 160 us -> 148 us
    pallas_call x1, Pallas kernels: 149 us -> 137 us  [run_mega(): pl.pallas_call(mega_kernel, in_specs=[anywhere, vmem, vmem, vmem, vmem, v...]
where the time goes in v3:
time: 161 us; the launch traced here: 160 us
  Pallas kernels  148 us (92%)
  local copies, waits for them, and re-layouts  5.16 us (3%)
  starting transfers between devices  3.37 us (2%)
    pallas_call x1, Pallas kernels, run_mega(): pl.pallas_call(mega_kernel, in_specs=[anywhere, vmem, vmem, vmem, vmem, v...  137 us
    pallas_call x1, Pallas kernels, gather_rows(): pl.pallas_call(functools.partial(gather_kernel, n_ids), grid_spec=pltpu.P...  11 us
    ppermute x1, starting transfers between devices, body(): ids_other = lax.ppermute(ids_mine, 'dp', swap)  3.37 us
  transfers between devices with their start and end apart: 1, of which 1 were waited for; matrix products, arithmetic and copies ran while one was open for 0% of the time, Pallas kernels for 0%

profile of v3, /device:TPU:0, one launch (start us, length us, event | category | flops | bytes accessed | tf_op | source)
XLA Modules:
  0.0 160.3 jit_solution(16383134242086546584)
XLA Ops:
  0.6 0.7 copy.22
  1.3 3.4 %collective-permute-start = (s32[2,129]{1,0:T(2,128)S(1)}, s32[2,129]{1,0:T(2,128)S(1)}, u32[]{:S(2)}, u32[]{:S(2)}) collective-permute-start(s32[2,129]{1,0:T(2,128)S(1)} %bitcast.19), channel_id=1, source_target_pairs={{0,4},{4,0},{1,5},{5,1},{2,6},{6,2},{3,7},{7,3}} | collective-permute-start | bytes 3104 | tf_op jit(solution)/shard_map/ppermute | solution.py:647
  4.7 0.1 fusion.11
  4.8 1.5 collective-permute-done
  6.3 0.1 and.19
  6.4 0.6 convert_reduce_fusion.count_ref
  7.0 0.1 min.12
  7.1 0.9 copy.17.sel_ref
  8.0 0.6 fusion.1.grp_ref
  8.5 11.0 %gather_rows.1.rows = bf16[4,136,2048]{2,1,0:T(8,128)(2,1)} custom-call(s32[1]{0:T(128)} %bitcast.flag_ref, s32[516]{0:T(1024)} %fusion.1.grp_ref, s32[4]{0:T(128)} %convert_reduce_fusion.count_ref, s32[4,136,1]{2,1,0:T(8,128)} %copy.17.sel_ref, bf16[25152,2048]{1,0:T(8,128)(2,1)} %bitcast.2.table_ref), custom_call_target="tpu_custom_call" | custom-call | flops 18396217344 | bytes 16908288 | tf_op jit(solution)/shard_map/gather_rows/pallas_call | solution.py:77
  19.6 0.8 broadcast_in_dim.14.tgt
  20.4 137.4 %mega.1 = f32[8,256]{1,0:T(8,128)} custom-call(bf16[4,136,2048]{2,1,0:T(8,128)(2,1)} %gather_rows.1.rows, s32[2,256,128]{2,1,0:T(8,128)} %broadcast_in_dim.14.tgt, bf16[2048]{0:T(1024)(128)(2,1)} %gain_f.1, bf16[2048]{0:T(1024)(128)(2,1)} %gain_h.1, bf16[2048]{0:T(1024)(128)(2,1)} %gain_e.1, bf16[2048]{0:T(1024)(128)(2,1)} %gain_m.1, ...), custom_call_target="tpu_custom_call" | custom-call | tf_op jit(solution)/shard_map/mega/pallas_call | solution.py:605
  157.8 1.3 slice_bitcast_fusion
  159.2 1.2 slice.21
  (4 shorter events, 0.0 us)
Async XLA Ops:
  1.3 4.9 %collective-permute-start = (s32[2,129]{1,0:T(2,128)S(1)}, s32[2,129]{1,0:T(2,128)S(1)}, u32[]{:S(2)}, u32[]{:S(2)}) collective-permute-start(s32[2,129]{1,0:T(2,128)S(1)} %bitcast.19), channel_id=1, source_target_pairs={{0,4},{4,0},{1,5},{5,1},{2,6},{6,2},{3,7},{7,3}} | collective-permute-start | bytes 3104 | tf_op jit(solution)/shard_map/ppermute | solution.py:647
